TPU v7x, 256 devices: a whole 4x4x8 slice. The times are simulated.
256 devices in a mesh: fft: 32 (over x_lo, z, core), scal: 8 (over x_hi, y).
Axes of the slice: x: 4 (x_hi: 2, x_lo: 2; x = x_hi * 2 + x_lo), y: 4, z: 8, core: 2. Of those that a mesh axis runs over, the one named last changes fastest.
Arguments:
- scalar_state: float32 [8, 2, 256, 256, 128], P('scal', None, 'fft'), may hold values from -12 to 12
- velocity: bfloat16 [3, 256, 256, 256], P(None, 'fft', 'scal'), may hold values from -6 to 6
- species: int32 [8], P('scal'), may hold values from 0 to 63
- kappa_table: float32 [64], replicated, may hold values from 0.1 to 1
- dealias_bound: int32 [8], P('scal'), may hold values from 64 to 85
Outputs:
- new_state: float32 [8, 2, 256, 256, 128], P('scal', None, 'fft')
- kappa: float32 [8], P('scal')
All inputs are finite; a program needn't handle non-finite values.
Results may differ from a plain program's by a relative error of at most 0.0027.
Values may be sent and summed in bfloat16 or wider, within the bound.
A program may use at most 128 MiB of HBM per device.

v0:
```python
import math
import jax
import jax.numpy as jnp
from jax import lax
from jax.sharding import PartitionSpec as P

cfl_number = 0.2


def in_one_piece(arrays, axis, split_dim, concat_dim, along):
    widths = [a.shape[along] for a in arrays]
    both = jnp.concatenate(arrays, axis=along)
    out = lax.all_to_all(both, axis, split_axis=split_dim, concat_axis=concat_dim, tiled=True)
    return tuple(jnp.split(out, [sum(widths[:k]) for k in range(1, len(widths))], axis=along))


def copy_for_each(x, axis):
    count = lax.axis_size(axis)
    return lax.all_to_all(jnp.broadcast_to(x[None], (count, *x.shape)), axis, 0, 0, tiled=True)


def collected_together(x, axis):
    leaves = jax.tree.leaves(x)
    sequence = sorted(range(len(leaves)), key=lambda k: -leaves[k].size)
    width = (1, *leaves[sequence[0]].shape)[-1]
    lines = [
        jnp.pad(leaves[k].reshape(-1), (0, -leaves[k].size % width)).reshape(-1, width)
        for k in sequence
    ]
    both, at, found = (copy_for_each(jnp.concatenate(lines), axis), 0, {})
    for k, line in zip(sequence, lines):
        section = both[:, at : at + len(line)].reshape(len(both), -1)
        found[k] = section[:, : leaves[k].size].reshape(-1, *leaves[k].shape)
        at += len(line)
    numbers = iter(range(len(leaves)))
    return jax.tree.map(lambda _: found[next(numbers)], x)


def folded_in_pairs(pieces, combine):
    while len(jax.tree.leaves(pieces)[0]) > 1:
        pieces = jax.vmap(combine)(
            *(jax.tree.map(lambda part: part[side::2], pieces) for side in (0, 1))
        )
    return jax.tree.map(lambda part: part[0], pieces)


def combined_all(x, axis, combine):
    pieces = collected_together(x, axis)
    return folded_in_pairs(pieces, combine)


def twiddle(size_in, size_out, length):
    row_index = jnp.arange(size_in, dtype=jnp.int32)[:, None]
    col_index = jnp.arange(size_out, dtype=jnp.int32)[None, :]
    angles = (row_index * col_index % length).astype(jnp.float32) * (2.0 * math.pi / length)
    norming = 1.0 / math.sqrt(length)
    return (jnp.cos(angles) * norming, jnp.sin(angles) * norming)


def build_tables(length):
    half_len = length // 2
    full_cos, full_sin = twiddle(length, length, length)
    inv_cos, inv_sin = twiddle(half_len, length, length)
    weight = jnp.where(jnp.arange(half_len, dtype=jnp.int32) == 0, 1.0, 2.0).astype(jnp.float32)[
        :, None
    ]
    fwd_cos, fwd_sin = twiddle(length, half_len, length)
    listed = (full_cos, full_sin, inv_cos * weight, inv_sin * weight, fwd_cos, fwd_sin)
    return tuple((matrix.astype(jnp.bfloat16) for matrix in listed))


def product(formula, operand, matrix):
    return jnp.einsum(formula, operand, matrix, preferred_element_type=jnp.float32)


def complex_section(real_part, imag_part, cos_matrix, sin_matrix, formula, inverse):
    real_cos = product(formula, real_part, cos_matrix)
    real_sin = product(formula, real_part, sin_matrix)
    imag_cos = product(formula, imag_part, cos_matrix)
    imag_sin = product(formula, imag_part, sin_matrix)
    if inverse:
        return (real_cos - imag_sin, real_sin + imag_cos)
    return (real_cos + imag_sin, imag_cos - real_sin)


def combine_stats(earlier, later):
    return (earlier[0] + later[0], earlier[1] + later[1], jnp.maximum(earlier[2], later[2]))


def times_wave(wavenumber, real_part, imag_part):
    new_real = (-wavenumber * imag_part.astype(jnp.float32)).astype(jnp.bfloat16)
    new_imag = (wavenumber * real_part.astype(jnp.float32)).astype(jnp.bfloat16)
    return (new_real, new_imag)


def body(scalar_state, velocity, species, kappa_table, dealias_bound):
    ky_local = scalar_state.shape[2]
    length = scalar_state.shape[3]
    half_len = length // 2
    total_count = kappa_table.shape[0]
    full_cos, full_sin, inv_cos, inv_sin, fwd_cos, fwd_sin = build_tables(length)
    ky_index = lax.axis_index("fft") * ky_local + jnp.arange(ky_local, dtype=jnp.int32)
    ky_wave = jnp.where(ky_index < half_len, ky_index, ky_index - length).astype(jnp.float32)[
        :, None, None
    ]
    kz_index = jnp.arange(length, dtype=jnp.int32)
    signed_full = jnp.where(kz_index < half_len, kz_index, kz_index - length).astype(jnp.float32)
    kz_wave = signed_full[None, :, None]
    ky_whole = signed_full[:, None, None]
    kx_wave = jnp.arange(half_len, dtype=jnp.int32).astype(jnp.float32)[None, None, :]
    ksquare = kx_wave * kx_wave + ky_wave * ky_wave + kz_wave * kz_wave
    weight = jnp.where(kx_wave == 0.0, 1.0, 2.0).astype(jnp.float32)
    cell_count = float(length) ** 3
    step_size = cfl_number * 2.0 * math.pi / length
    speeds = lax.all_gather(velocity, "scal", axis=2, tiled=True)

    def finish_inverse(halves):
        y_section = complex_section(
            halves[0], halves[1], full_cos, full_sin, "...yzx,yw->...zwx", True
        )
        y_real = y_section[0].astype(jnp.bfloat16)
        y_imag = y_section[1].astype(jnp.bfloat16)
        return product("...zwk,kx->...zwx", y_real, inv_cos) - product(
            "...zwk,kx->...zwx", y_imag, inv_sin
        )

    def gradient_set(real_part, imag_part):
        pair_real = jnp.stack([real_part, -kz_wave * imag_part]).astype(jnp.bfloat16)
        pair_imag = jnp.stack([imag_part, kz_wave * real_part]).astype(jnp.bfloat16)
        z_section = complex_section(
            pair_real, pair_imag, full_cos, full_sin, "...ykx,kz->...yzx", True
        )
        z_real = z_section[0].astype(jnp.bfloat16)
        z_imag = z_section[1].astype(jnp.bfloat16)
        came_real, came_imag = in_one_piece((z_real, z_imag), "fft", 2, 1, 0)
        x_real, x_imag = times_wave(kx_wave, came_real[0], came_imag[0])
        y_real, y_imag = times_wave(ky_whole, came_real[0], came_imag[0])
        all_real = jnp.stack([x_real, y_real, came_real[1]])
        all_imag = jnp.stack([x_imag, y_imag, came_imag[1]])
        return finish_inverse((all_real, all_imag))

    def advect(gradients):
        total = speeds[0].astype(jnp.float32) * gradients[0]
        total = total + speeds[1].astype(jnp.float32) * gradients[1]
        total = total + speeds[2].astype(jnp.float32) * gradients[2]
        return total.astype(jnp.bfloat16)

    def finish_forward(halves):
        return complex_section(halves[0], halves[1], full_cos, full_sin, "...wzk,zv->...wvk", False)

    def tendency(advected, bound):
        real_x = product("zyx,xk->zyk", advected, fwd_cos).astype(jnp.bfloat16)
        imag_x = (-product("zyx,xk->zyk", advected, fwd_sin)).astype(jnp.bfloat16)
        y_section = complex_section(real_x, imag_x, full_cos, full_sin, "zyk,yw->wzk", False)
        y_real = y_section[0].astype(jnp.bfloat16)
        y_imag = y_section[1].astype(jnp.bfloat16)
        spectral = finish_forward(
            (
                lax.all_to_all(y_real, "fft", split_axis=0, concat_axis=1, tiled=True),
                lax.all_to_all(y_imag, "fft", split_axis=0, concat_axis=1, tiled=True),
            )
        )
        dealias_mask = (ksquare <= bound * bound).astype(jnp.float32)
        return (-dealias_mask * spectral[0], -dealias_mask * spectral[1])

    scalar = 0
    start_real = scalar_state[scalar, 0]
    start_imag = scalar_state[scalar, 1]
    energy = start_real * start_real + start_imag * start_imag
    local_var = [jnp.sum(weight * energy) / cell_count]
    local_grad = [jnp.sum(weight * ksquare * energy) / cell_count]
    gradients = gradient_set(start_real, start_imag)
    magnitude = jnp.sqrt(
        gradients[0] * gradients[0] + gradients[1] * gradients[1] + gradients[2] * gradients[2]
    )
    local_peak = [jnp.max(magnitude)]
    advect_saved = [advect(gradients)]
    var_part = jnp.stack(local_var)
    grad_part = jnp.stack(local_grad)
    peak_part = jnp.stack(local_peak)
    variance, mean_grad, peak_value = combined_all(
        (var_part, grad_part, peak_part), "fft", combine_stats
    )
    matches = species[:, None] == jnp.arange(total_count, dtype=jnp.int32)[None, :]
    base_kappa = jnp.sum(jnp.where(matches, kappa_table[None, :], 0.0), axis=1)
    kappa = base_kappa * peak_value * jnp.sqrt(variance) / (mean_grad + 1e-06)
    scalar = 0
    start_real = scalar_state[scalar, 0]
    start_imag = scalar_state[scalar, 1]
    factor = jnp.exp(-kappa[scalar] * ksquare * step_size)
    bound = dealias_bound[scalar].astype(jnp.float32)
    first_real, first_imag = tendency(advect_saved[scalar], bound)
    mid_real = factor * (start_real + step_size * first_real)
    mid_imag = factor * (start_imag + step_size * first_imag)
    second_real, second_imag = tendency(advect(gradient_set(mid_real, mid_imag)), bound)
    new_real = factor * start_real + 0.5 * step_size * (factor * first_real + second_real)
    new_imag = factor * start_imag + 0.5 * step_size * (factor * first_imag + second_imag)
    updated_list = [jnp.stack([new_real, new_imag])]
    return (jnp.stack(updated_list), kappa)


def solution(mesh):
    placed = (
        P("scal", None, "fft", None, None),
        P(None, "fft", "scal", None),
        P("scal"),
        P(),
        P("scal"),
    )
    return jax.shard_map(
        body,
        mesh=mesh,
        in_specs=placed,
        out_specs=(P("scal", None, "fft", None, None), P("scal")),
        check_vma=False,
    )
```

profile of v0, /device:TPU:1, one launch (start us, length us, event | category | flops | bytes accessed | tf_op | source)
XLA Modules:
  0.0 341.0 jit_solution(12632958124329488233)
XLA Ops:
  18.0 11.1 %all-to-all-start = ((bf16[4,8,256,128]{3,1,0,2:T(8,128)(2,1)}), bf16[4,8,256,128]{3,1,0,2:T(8,128)(2,1)}, u32[]{:S(2)}, u32[]{:S(2)}) async-start(bf16[4,8,256,128]{3,1,0,2:T(8,128)(2,1)} %copy.71), calls=%async_computation | async-start | bytes 4194304 | tf_op jit(solution)/shard_map/all_to_all | solution.py:13
  32.1 46.3 %all-to-all-done = bf16[4,8,256,128]{3,1,0,2:T(8,128)(2,1)} async-done(((bf16[4,8,256,128]{3,1,0,2:T(8,128)(2,1)}), bf16[4,8,256,128]{3,1,0,2:T(8,128)(2,1)}, u32[]{:S(2)}, u32[]{:S(2)}) %all-to-all-start) | async-done | bytes 2097184 | tf_op jit(solution)/shard_map/all_to_all | solution.py:13
  82.1 3.1 fusion.60
  85.2 3.1 fusion.59
  89.4 7.1 %fusion.10 = f32[3,8,256,256]{3,2,1,0:T(8,128)} fusion(f32[256,3,8,128]{3,0,2,1:T(8,128)} %fusion.60, bf16[1,256,8,128]{3,1,2,0:T(8,128)(2,1)S(1)} %copy.82, bf16[1,256,8,128]{3,1,2,0:T(8,128)(2,1)} %get-tuple-element.32, bf16[1,256,8,128]{3,1,2,0:T(8,128)(2,1)S(1)} %get-tuple-element.31, f32[128]{0:T(128)S(1)} %fusion.155), kind=kOutput, calls=%fused_computation.39 | convolution fusion | flops 813170688 | bytes 11010560 | tf_op jit(solution)/shard_map/...zwk,kx->...zwx/dot_general | solution.py:73
  96.5 9.0 %convolution_subtract_fusion.1 = f32[3,8,256,256]{3,2,1,0:T(8,128)} fusion(f32[3,8,256,256]{3,2,1,0:T(8,128)} %fusion.10, f32[256,3,8,128]{3,0,2,1:T(8,128)} %fusion.59, bf16[1,256,8,128]{3,1,2,0:T(8,128)(2,1)S(1)} %copy.82, bf16[1,256,8,128]{3,1,2,0:T(8,128)(2,1)} %get-tuple-element.32, bf16[1,256,8,128]{3,1,2,0:T(8,128)(2,1)S(1)} %get-tuple-element.31, ...), kind=kOutput, calls=%fused_computation.5 | convolution fusion | flops 814743552 | bytes 17302016 | tf_op jit(solution)/shard_map/...zwk,kx->...zwx/dot_general | solution.py:73
  105.5 5.7 %sqrt_reduce_fusion = (f32[]{:T(128)}, bf16[8,256,256]{2,1,0:T(8,128)(2,1)S(1)}) fusion(f32[3,8,256,256]{3,2,1,0:T(8,128)} %convolution_subtract_fusion.1, bf16[3,8,256,256]{3,2,1,0:T(8,128)(2,1)} %all-gather.2.cloned.1.call-done), kind=kLoop, calls=%fused_computation.23 | loop fusion | flops 7864319 | bytes 10485764 | tf_op jit(solution)/shard_map/reduce_max | solution.py:176
  116.9 6.6 %all-to-all-start.1 = ((f32[32,3,1]{1,2,0:T(1,128)}), f32[32,3,1]{1,2,0:T(1,128)S(1)}, u32[]{:S(2)}, u32[]{:S(2)}) async-start(f32[32,3,1]{1,2,0:T(1,128)} %broadcast_in_dim.23), calls=%async_computation.1 | async-start | bytes 32768 | tf_op jit(solution)/shard_map/all_to_all | solution.py:19
  126.9 4.5 %all-to-all-done.1 = f32[32,3,1]{1,2,0:T(1,128)S(1)} async-done(((f32[32,3,1]{1,2,0:T(1,128)}), f32[32,3,1]{1,2,0:T(1,128)S(1)}, u32[]{:S(2)}, u32[]{:S(2)}) %all-to-all-start.1) | async-done | bytes 416 | tf_op jit(solution)/shard_map/all_to_all | solution.py:19
  131.4 4.3 %all-to-all-start.3 = ((bf16[256,8,128]{2,1,0:T(8,128)(2,1)}), bf16[256,8,128]{2,1,0:T(8,128)(2,1)S(1)}, u32[]{:S(2)}, u32[]{:S(2)}) async-start(bf16[256,8,128]{2,1,0:T(8,128)(2,1)} %copy.85), calls=%async_computation.3 | async-start | bytes 1048576 | tf_op jit(solution)/shard_map/all_to_all | solution.py:160
  140.4 12.1 %all-to-all-done.3 = bf16[256,8,128]{2,1,0:T(8,128)(2,1)S(1)} async-done(((bf16[256,8,128]{2,1,0:T(8,128)(2,1)}), bf16[256,8,128]{2,1,0:T(8,128)(2,1)S(1)}, u32[]{:S(2)}, u32[]{:S(2)}) %all-to-all-start.3) | async-done | bytes 524320 | tf_op jit(solution)/shard_map/all_to_all | solution.py:160
  152.5 5.8 %all-to-all-start.2 = ((bf16[256,8,128]{2,1,0:T(8,128)(2,1)}), bf16[256,8,128]{2,1,0:T(8,128)(2,1)S(1)}, u32[]{:S(2)}, u32[]{:S(2)}) async-start(bf16[256,8,128]{2,1,0:T(8,128)(2,1)} %copy.83), calls=%async_computation.2 | async-start | bytes 1048576 | tf_op jit(solution)/shard_map/all_to_all | solution.py:159
  187.9 54.4 %all_to_all.107 = bf16[4,8,256,128]{3,1,0,2:T(8,128)(2,1)S(1)} all-to-all(bf16[4,8,256,128]{3,1,0,2:T(8,128)(2,1)S(1)} %copy.87), channel_id=1, replica_groups=mesh['fft'=32,'scal'=8] {'fft'}, dimensions={2} | all-to-all | bytes 4194304 | tf_op jit(solution)/shard_map/all_to_all | solution.py:13
  244.0 3.1 fusion.58
  247.1 3.1 fusion.57
  251.7 7.1 %fusion.7 = f32[3,8,256,256]{3,2,1,0:T(8,128)} fusion(f32[256,3,8,128]{3,0,2,1:T(8,128)} %fusion.58, bf16[1,256,8,128]{3,1,2,0:T(8,128)(2,1)S(1)} %copy.98, bf16[1,256,8,128]{3,1,2,0:T(8,128)(2,1)} %get-tuple-element.28, bf16[1,256,8,128]{3,1,2,0:T(8,128)(2,1)S(1)} %get-tuple-element.27, f32[128]{0:T(128)S(1)} %fusion.155), kind=kOutput, calls=%fused_computation.36 | convolution fusion | flops 813170688 | bytes 11010560 | tf_op jit(solution)/shard_map/...zwk,kx->...zwx/dot_general | solution.py:73
  258.8 8.9 %convolution_subtract_fusion = f32[3,8,256,256]{3,2,1,0:T(8,128)} fusion(f32[3,8,256,256]{3,2,1,0:T(8,128)} %fusion.7, f32[256,3,8,128]{3,0,2,1:T(8,128)} %fusion.57, bf16[1,256,8,128]{3,1,2,0:T(8,128)(2,1)S(1)} %copy.98, bf16[1,256,8,128]{3,1,2,0:T(8,128)(2,1)} %get-tuple-element.28, bf16[1,256,8,128]{3,1,2,0:T(8,128)(2,1)S(1)} %get-tuple-element.27, ...), kind=kOutput, calls=%fused_computation.4 | convolution fusion | flops 814743552 | bytes 17302016 | tf_op jit(solution)/shard_map/...zwk,kx->...zwx/dot_general | solution.py:73
  267.7 4.5 %fusion.48 = bf16[8,256,256]{2,1,0:T(8,128)(2,1)S(1)} fusion(f32[3,8,256,256]{3,2,1,0:T(8,128)} %convolution_subtract_fusion, bf16[3,8,256,256]{3,2,1,0:T(8,128)(2,1)} %all-gather.2.cloned.1.call-done), kind=kLoop, calls=%fused_computation.89 | loop fusion | flops 4718592 | bytes 10485760 | tf_op jit(solution)/shard_map/add | solution.py:145
  278.0 5.9 %all-to-all-start.6 = ((bf16[256,8,128]{2,1,0:T(8,128)(2,1)}), bf16[256,8,128]{2,1,0:T(8,128)(2,1)S(1)}, u32[]{:S(2)}, u32[]{:S(2)}) async-start(bf16[256,8,128]{2,1,0:T(8,128)(2,1)} %copy.101), calls=%async_computation.6 | async-start | bytes 1048576 | tf_op jit(solution)/shard_map/all_to_all | solution.py:160
  288.5 12.0 %all-to-all-done.6 = bf16[256,8,128]{2,1,0:T(8,128)(2,1)S(1)} async-done(((bf16[256,8,128]{2,1,0:T(8,128)(2,1)}), bf16[256,8,128]{2,1,0:T(8,128)(2,1)S(1)}, u32[]{:S(2)}, u32[]{:S(2)}) %all-to-all-start.6) | async-done | bytes 524320 | tf_op jit(solution)/shard_map/all_to_all | solution.py:160
  301.3 6.6 %all-to-all-start.5 = ((bf16[256,8,128]{2,1,0:T(8,128)(2,1)}), bf16[256,8,128]{2,1,0:T(8,128)(2,1)}, u32[]{:S(2)}, u32[]{:S(2)}) async-start(bf16[256,8,128]{2,1,0:T(8,128)(2,1)} %copy.99), calls=%async_computation.5 | async-start | bytes 1048576 | tf_op jit(solution)/shard_map/all_to_all | solution.py:159
  307.9 3.3 fusion.66
  311.2 13.2 %all-to-all-done.5 = bf16[256,8,128]{2,1,0:T(8,128)(2,1)} async-done(((bf16[256,8,128]{2,1,0:T(8,128)(2,1)}), bf16[256,8,128]{2,1,0:T(8,128)(2,1)}, u32[]{:S(2)}, u32[]{:S(2)}) %all-to-all-start.5) | async-done | bytes 524320 | tf_op jit(solution)/shard_map/all_to_all | solution.py:159
  326.7 3.0 fusion.21
  (138 shorter events, 74.0 us)
Async XLA Ops:
  7.2 2.2 copy-start
  18.0 60.4 %all-to-all-start = ((bf16[4,8,256,128]{3,1,0,2:T(8,128)(2,1)}), bf16[4,8,256,128]{3,1,0,2:T(8,128)(2,1)}, u32[]{:S(2)}, u32[]{:S(2)}) async-start(bf16[4,8,256,128]{3,1,0,2:T(8,128)(2,1)} %copy.71), calls=%async_computation | async-start | bytes 4194304 | tf_op jit(solution)/shard_map/all_to_all | solution.py:13
  29.1 76.4 %all-gather.2.cloned.1.call-start = ((), (), s32[]{:S(2)}) async-start(), calls=%async_computation.7 | async-start | bytes 3538944 | tf_op jit(solution)/shard_map/all_gather | solution.py:115
  112.7 1.7 copy-start.7
  116.9 14.5 %all-to-all-start.1 = ((f32[32,3,1]{1,2,0:T(1,128)}), f32[32,3,1]{1,2,0:T(1,128)S(1)}, u32[]{:S(2)}, u32[]{:S(2)}) async-start(f32[32,3,1]{1,2,0:T(1,128)} %broadcast_in_dim.23), calls=%async_computation.1 | async-start | bytes 32768 | tf_op jit(solution)/shard_map/all_to_all | solution.py:19
  125.8 12.2 %copy-start.8 = (bf16[8,256,128]{2,1,0:T(8,128)(2,1)S(1)}, bf16[8,256,128]{2,1,0:T(8,128)(2,1)}, u32[]{:S(2)}) copy-start(bf16[8,256,128]{2,1,0:T(8,128)(2,1)} %copy-done.7) | copy-start | bytes 1572868
  131.4 21.0 %all-to-all-start.3 = ((bf16[256,8,128]{2,1,0:T(8,128)(2,1)}), bf16[256,8,128]{2,1,0:T(8,128)(2,1)S(1)}, u32[]{:S(2)}, u32[]{:S(2)}) async-start(bf16[256,8,128]{2,1,0:T(8,128)(2,1)} %copy.85), calls=%async_computation.3 | async-start | bytes 1048576 | tf_op jit(solution)/shard_map/all_to_all | solution.py:160
  138.0 21.5 %copy-start.10 = (f32[64]{0:T(128)S(1)}, f32[64]{0:T(128)}, u32[]{:S(2)}) copy-start(f32[64]{0:T(128)} %param.8) | copy-start | bytes 772
  152.5 22.3 %all-to-all-start.2 = ((bf16[256,8,128]{2,1,0:T(8,128)(2,1)}), bf16[256,8,128]{2,1,0:T(8,128)(2,1)S(1)}, u32[]{:S(2)}, u32[]{:S(2)}) async-start(bf16[256,8,128]{2,1,0:T(8,128)(2,1)} %copy.83), calls=%async_computation.2 | async-start | bytes 1048576 | tf_op jit(solution)/shard_map/all_to_all | solution.py:159
  178.5 2.1 copy-start.3
  179.7 1.0 copy-start.1
  274.4 2.4 copy-start.9
  278.0 22.5 %all-to-all-start.6 = ((bf16[256,8,128]{2,1,0:T(8,128)(2,1)}), bf16[256,8,128]{2,1,0:T(8,128)(2,1)S(1)}, u32[]{:S(2)}, u32[]{:S(2)}) async-start(bf16[256,8,128]{2,1,0:T(8,128)(2,1)} %copy.101), calls=%async_computation.6 | async-start | bytes 1048576 | tf_op jit(solution)/shard_map/all_to_all | solution.py:160
  300.5 0.8 copy-start.5
  301.3 23.2 %all-to-all-start.5 = ((bf16[256,8,128]{2,1,0:T(8,128)(2,1)}), bf16[256,8,128]{2,1,0:T(8,128)(2,1)}, u32[]{:S(2)}, u32[]{:S(2)}) async-start(bf16[256,8,128]{2,1,0:T(8,128)(2,1)} %copy.99), calls=%async_computation.5 | async-start | bytes 1048576 | tf_op jit(solution)/shard_map/all_to_all | solution.py:159
  307.9 18.8 %copy-start.4 = (f32[8,256,128]{2,1,0:T(8,128)S(1)}, f32[8,256,128]{2,1,0:T(8,128)}, u32[]{:S(2)}) copy-start(f32[8,256,128]{2,1,0:T(8,128)} %copy-done.3) | copy-start | bytes 3145732
  326.7 3.1 copy-start.2
  326.7 3.1 copy-start.6
Sparse Core Ops, SparseCore 0:
  32.5 72.3 all-gather.1
where the time goes:
time: 348 us; the launch traced here: 341 us
  waiting for transfers between devices  91.2 us (26%)
  matrix products  90.6 us (26%)
  blocking collectives  54.4 us (16%)
  starting transfers between devices  40.6 us (12%)
  between operations  23 us (7%)
  local copies, waits for them, and re-layouts  21.8 us (6%)
  other arithmetic  19.3 us (6%)
    dot_general x36, matrix products, product(): jnp.einsum(formula, operand, matrix, preferred_element_type=jnp.float32)  90.6 us
    all_to_all x1, blocking collectives, in_one_piece(): lax.all_to_all(both, axis, split_axis=split_dim, concat_axis=concat_dim,...  54.4 us
    all_to_all x1, waiting for transfers between devices, in_one_piece(): lax.all_to_all(both, axis, split_axis=split_dim, concat_axis=concat_dim,...  46.3 us
    all_to_all x2, waiting for transfers between devices, tendency(): lax.all_to_all(y_imag, 'fft', split_axis=0, concat_axis=1, tiled=True)  24.1 us
    all_to_all x2, waiting for transfers between devices, tendency(): lax.all_to_all(y_real, 'fft', split_axis=0, concat_axis=1, tiled=True)  16 us
    all_to_all x2, starting transfers between devices, tendency(): lax.all_to_all(y_real, 'fft', split_axis=0, concat_axis=1, tiled=True)  12.4 us
    all_to_all x1, starting transfers between devices, in_one_piece(): lax.all_to_all(both, axis, split_axis=split_dim, concat_axis=concat_dim,...  11.1 us
    all_to_all x2, starting transfers between devices, tendency(): lax.all_to_all(y_imag, 'fft', split_axis=0, concat_axis=1, tiled=True)  10.2 us
  transfers between devices with their start and end apart: 7, of which 6 were waited for; matrix products, arithmetic and copies ran while one was open for 15% of the time, Pallas kernels for 0%

commit v1 on v0

--- a/solution.py
+++ b/solution.py
@@ -3,8 +3,17 @@
 import jax.numpy as jnp
 from jax import lax
 from jax.sharding import PartitionSpec as P
+from jax.lax import all_to_all, axis_size
 
 cfl_number = 0.2
+
+
+def perform_entries(x_local, dev_axis):
+    reply = axis_size(dev_axis)
+    h_now = jnp.split(x_local, reply, axis=0)
+    y = jnp.stack(h_now)
+    current_arr = all_to_all(y, axis_name=dev_axis, split_axis=0, concat_axis=0)
+    return jnp.concatenate(current_arr, axis=1)
 
 
 def in_one_piece(arrays, axis, split_dim, concat_dim, along):
@@ -157,7 +166,7 @@
         spectral = finish_forward(
             (
                 lax.all_to_all(y_real, "fft", split_axis=0, concat_axis=1, tiled=True),
-                lax.all_to_all(y_imag, "fft", split_axis=0, concat_axis=1, tiled=True),
+                perform_entries(y_imag, "fft"),
             )
         )
         dealias_mask = (ksquare <= bound * bound).astype(jnp.float32)

time: 348 us -> 386 us (1.11)
  local copies, waits for them, and re-layouts: 21.8 us -> 58.7 us
    unnamed x22 -> x82, local copies, waits for them, and re-layouts: 1.24 us -> 39.1 us
  transfers between devices with their start and end apart: 7 -> 7, of which waited for: 6 -> 6; matrix products, arithmetic and copies ran while one was open for 15% -> 13% of each run, Pallas kernels for 0% -> 0%
where the time goes in v1:
time: 386 us; the launch traced here: 379 us
  waiting for transfers between devices  93.7 us (24%)
  matrix products  89 us (23%)
  local copies, waits for them, and re-layouts  58.7 us (15%)
  blocking collectives  54.5 us (14%)
  starting transfers between devices  40.6 us (11%)
  between operations  23.2 us (6%)
  other arithmetic  19.1 us (5%)
    dot_general x36, matrix products, product(): jnp.einsum(formula, operand, matrix, preferred_element_type=jnp.float32)  89 us
    all_to_all x1, blocking collectives, in_one_piece(): lax.all_to_all(both, axis, split_axis=split_dim, concat_axis=concat_dim,...  54.5 us
    all_to_all x1, waiting for transfers between devices, in_one_piece(): lax.all_to_all(both, axis, split_axis=split_dim, concat_axis=concat_dim,...  46.1 us
    unnamed x82, local copies, waits for them, and re-layouts  39.1 us
    all_to_all x2, waiting for transfers between devices, perform_entries(): current_arr = all_to_all(y, axis_name=dev_axis, split_axis=0, concat_axis=0)  24.1 us
    all_to_all x2, waiting for transfers between devices, tendency(): lax.all_to_all(y_real, 'fft', split_axis=0, concat_axis=1, tiled=True)  15.9 us
    all_to_all x2, starting transfers between devices, tendency(): lax.all_to_all(y_real, 'fft', split_axis=0, concat_axis=1, tiled=True)  12.4 us
    all_to_all x1, starting transfers between devices, in_one_piece(): lax.all_to_all(both, axis, split_axis=split_dim, concat_axis=concat_dim,...  11.1 us
  transfers between devices with their start and end apart: 7, of which 6 were waited for; matrix products, arithmetic and copies ran while one was open for 13% of the time, Pallas kernels for 0%

profile of v1, /device:TPU:1, one launch (start us, length us, event | category | flops | bytes accessed | tf_op | source)
XLA Modules:
  0.0 378.9 jit_solution(11076963881745123262)
XLA Ops:
  18.0 11.1 %all-to-all-start = ((bf16[4,8,256,128]{3,1,0,2:T(8,128)(2,1)}), bf16[4,8,256,128]{3,1,0,2:T(8,128)(2,1)}, u32[]{:S(2)}, u32[]{:S(2)}) async-start(bf16[4,8,256,128]{3,1,0,2:T(8,128)(2,1)} %copy.75), calls=%async_computation | async-start | bytes 4194304 | tf_op jit(solution)/shard_map/all_to_all | solution.py:22
  32.3 46.1 %all-to-all-done = bf16[4,8,256,128]{3,1,0,2:T(8,128)(2,1)} async-done(((bf16[4,8,256,128]{3,1,0,2:T(8,128)(2,1)}), bf16[4,8,256,128]{3,1,0,2:T(8,128)(2,1)}, u32[]{:S(2)}, u32[]{:S(2)}) %all-to-all-start) | async-done | bytes 2097184 | tf_op jit(solution)/shard_map/all_to_all | solution.py:22
  82.1 3.1 fusion.60
  85.2 3.1 fusion.59
  89.5 7.1 %fusion.10 = f32[3,8,256,256]{3,2,1,0:T(8,128)} fusion(f32[256,3,8,128]{3,0,2,1:T(8,128)} %fusion.60, bf16[1,256,8,128]{3,1,2,0:T(8,128)(2,1)S(1)} %copy.86, bf16[1,256,8,128]{3,1,2,0:T(8,128)(2,1)} %get-tuple-element.32, bf16[1,256,8,128]{3,1,2,0:T(8,128)(2,1)S(1)} %get-tuple-element.31, f32[128]{0:T(128)S(1)} %fusion.151), kind=kOutput, calls=%fused_computation.39 | convolution fusion | flops 813170688 | bytes 11010560 | tf_op jit(solution)/shard_map/...zwk,kx->...zwx/dot_general | solution.py:82
  96.5 9.0 %convolution_subtract_fusion.1 = f32[3,8,256,256]{3,2,1,0:T(8,128)} fusion(f32[3,8,256,256]{3,2,1,0:T(8,128)} %fusion.10, f32[256,3,8,128]{3,0,2,1:T(8,128)} %fusion.59, bf16[1,256,8,128]{3,1,2,0:T(8,128)(2,1)S(1)} %copy.86, bf16[1,256,8,128]{3,1,2,0:T(8,128)(2,1)} %get-tuple-element.32, bf16[1,256,8,128]{3,1,2,0:T(8,128)(2,1)S(1)} %get-tuple-element.31, ...), kind=kOutput, calls=%fused_computation.5 | convolution fusion | flops 814743552 | bytes 17302016 | tf_op jit(solution)/shard_map/...zwk,kx->...zwx/dot_general | solution.py:82
  105.5 5.7 %sqrt_reduce_fusion = (f32[]{:T(128)}, bf16[8,256,256]{2,1,0:T(8,128)(2,1)S(1)}) fusion(f32[3,8,256,256]{3,2,1,0:T(8,128)} %convolution_subtract_fusion.1, bf16[3,8,256,256]{3,2,1,0:T(8,128)(2,1)} %all-gather.2.cloned.1.call-done), kind=kLoop, calls=%fused_computation.23 | loop fusion | flops 7864319 | bytes 10485764 | tf_op jit(solution)/shard_map/reduce_max | solution.py:185
  136.3 6.6 %all-to-all-start.1 = ((f32[32,3,1]{1,2,0:T(1,128)}), f32[32,3,1]{1,2,0:T(1,128)S(1)}, u32[]{:S(2)}, u32[]{:S(2)}) async-start(f32[32,3,1]{1,2,0:T(1,128)} %broadcast_in_dim.23), calls=%async_computation.1 | async-start | bytes 32768 | tf_op jit(solution)/shard_map/all_to_all | solution.py:28
  143.5 7.3 %all-to-all-done.1 = f32[32,3,1]{1,2,0:T(1,128)S(1)} async-done(((f32[32,3,1]{1,2,0:T(1,128)}), f32[32,3,1]{1,2,0:T(1,128)S(1)}, u32[]{:S(2)}, u32[]{:S(2)}) %all-to-all-start.1) | async-done | bytes 416 | tf_op jit(solution)/shard_map/all_to_all | solution.py:28
  150.8 4.3 %all-to-all-start.3 = ((bf16[32,8,8,128]{3,1,2,0:T(8,128)(2,1)}), bf16[32,8,8,128]{3,1,2,0:T(8,128)(2,1)S(1)}, u32[]{:S(2)}, u32[]{:S(2)}) async-start(bf16[32,8,8,128]{3,1,2,0:T(8,128)(2,1)} %constant_dynamic-update-slice_fusion), calls=%async_computation.3 | async-start | bytes 1048576 | tf_op jit(solution)/shard_map/all_to_all | solution.py:15
  159.7 12.1 %all-to-all-done.3 = bf16[32,8,8,128]{3,1,2,0:T(8,128)(2,1)S(1)} async-done(((bf16[32,8,8,128]{3,1,2,0:T(8,128)(2,1)}), bf16[32,8,8,128]{3,1,2,0:T(8,128)(2,1)S(1)}, u32[]{:S(2)}, u32[]{:S(2)}) %all-to-all-start.3) | async-done | bytes 524320 | tf_op jit(solution)/shard_map/all_to_all | solution.py:15
  171.8 5.8 %all-to-all-start.2 = ((bf16[256,8,128]{2,1,0:T(8,128)(2,1)}), bf16[256,8,128]{2,1,0:T(8,128)(2,1)S(1)}, u32[]{:S(2)}, u32[]{:S(2)}) async-start(bf16[256,8,128]{2,1,0:T(8,128)(2,1)} %copy.87), calls=%async_computation.2 | async-start | bytes 1048576 | tf_op jit(solution)/shard_map/all_to_all | solution.py:168
  207.2 54.5 %all_to_all.81 = bf16[4,8,256,128]{3,1,0,2:T(8,128)(2,1)S(1)} all-to-all(bf16[4,8,256,128]{3,1,0,2:T(8,128)(2,1)S(1)} %copy.91), channel_id=1, replica_groups=mesh['fft'=32,'scal'=8] {'fft'}, dimensions={2} | all-to-all | bytes 4194304 | tf_op jit(solution)/shard_map/all_to_all | solution.py:22
  263.5 3.1 fusion.58
  266.6 3.1 fusion.57
  271.2 7.1 %fusion.7 = f32[3,8,256,256]{3,2,1,0:T(8,128)} fusion(f32[256,3,8,128]{3,0,2,1:T(8,128)} %fusion.58, bf16[1,256,8,128]{3,1,2,0:T(8,128)(2,1)S(1)} %copy.102, bf16[1,256,8,128]{3,1,2,0:T(8,128)(2,1)} %get-tuple-element.28, bf16[1,256,8,128]{3,1,2,0:T(8,128)(2,1)S(1)} %get-tuple-element.27, f32[128]{0:T(128)S(1)} %fusion.151), kind=kOutput, calls=%fused_computation.36 | convolution fusion | flops 813170688 | bytes 11010560 | tf_op jit(solution)/shard_map/...zwk,kx->...zwx/dot_general | solution.py:82
  278.3 8.9 %convolution_subtract_fusion = f32[3,8,256,256]{3,2,1,0:T(8,128)} fusion(f32[3,8,256,256]{3,2,1,0:T(8,128)} %fusion.7, f32[256,3,8,128]{3,0,2,1:T(8,128)} %fusion.57, bf16[1,256,8,128]{3,1,2,0:T(8,128)(2,1)S(1)} %copy.102, bf16[1,256,8,128]{3,1,2,0:T(8,128)(2,1)} %get-tuple-element.28, bf16[1,256,8,128]{3,1,2,0:T(8,128)(2,1)S(1)} %get-tuple-element.27, ...), kind=kOutput, calls=%fused_computation.4 | convolution fusion | flops 814743552 | bytes 17302016 | tf_op jit(solution)/shard_map/...zwk,kx->...zwx/dot_general | solution.py:82
  287.2 4.5 %fusion.48 = bf16[8,256,256]{2,1,0:T(8,128)(2,1)S(1)} fusion(f32[3,8,256,256]{3,2,1,0:T(8,128)} %convolution_subtract_fusion, bf16[3,8,256,256]{3,2,1,0:T(8,128)(2,1)} %all-gather.2.cloned.1.call-done), kind=kLoop, calls=%fused_computation.89 | loop fusion | flops 4718592 | bytes 10485760 | tf_op jit(solution)/shard_map/add | solution.py:154
  315.9 5.9 %all-to-all-start.6 = ((bf16[32,8,8,128]{3,1,2,0:T(8,128)(2,1)}), bf16[32,8,8,128]{3,1,2,0:T(8,128)(2,1)S(1)}, u32[]{:S(2)}, u32[]{:S(2)}) async-start(bf16[32,8,8,128]{3,1,2,0:T(8,128)(2,1)} %constant_dynamic-update-slice_fusion.32), calls=%async_computation.6 | async-start | bytes 1048576 | tf_op jit(solution)/shard_map/all_to_all | solution.py:15
  326.4 12.0 %all-to-all-done.6 = bf16[32,8,8,128]{3,1,2,0:T(8,128)(2,1)S(1)} async-done(((bf16[32,8,8,128]{3,1,2,0:T(8,128)(2,1)}), bf16[32,8,8,128]{3,1,2,0:T(8,128)(2,1)S(1)}, u32[]{:S(2)}, u32[]{:S(2)}) %all-to-all-start.6) | async-done | bytes 524320 | tf_op jit(solution)/shard_map/all_to_all | solution.py:15
  339.2 6.6 %all-to-all-start.5 = ((bf16[256,8,128]{2,1,0:T(8,128)(2,1)}), bf16[256,8,128]{2,1,0:T(8,128)(2,1)}, u32[]{:S(2)}, u32[]{:S(2)}) async-start(bf16[256,8,128]{2,1,0:T(8,128)(2,1)} %copy.103), calls=%async_computation.5 | async-start | bytes 1048576 | tf_op jit(solution)/shard_map/all_to_all | solution.py:168
  345.8 3.3 fusion.69
  349.2 13.2 %all-to-all-done.5 = bf16[256,8,128]{2,1,0:T(8,128)(2,1)} async-done(((bf16[256,8,128]{2,1,0:T(8,128)(2,1)}), bf16[256,8,128]{2,1,0:T(8,128)(2,1)}, u32[]{:S(2)}, u32[]{:S(2)}) %all-to-all-start.5) | async-done | bytes 524320 | tf_op jit(solution)/shard_map/all_to_all | solution.py:168
  364.7 3.0 fusion.21
  (198 shorter events, 109.0 us)
Async XLA Ops:
  7.2 2.2 copy-start
  18.0 60.4 %all-to-all-start = ((bf16[4,8,256,128]{3,1,0,2:T(8,128)(2,1)}), bf16[4,8,256,128]{3,1,0,2:T(8,128)(2,1)}, u32[]{:S(2)}, u32[]{:S(2)}) async-start(bf16[4,8,256,128]{3,1,0,2:T(8,128)(2,1)} %copy.75), calls=%async_computation | async-start | bytes 4194304 | tf_op jit(solution)/shard_map/all_to_all | solution.py:22
  29.1 76.5 %all-gather.2.cloned.1.call-start = ((), (), s32[]{:S(2)}) async-start(), calls=%async_computation.7 | async-start | bytes 3538944 | tf_op jit(solution)/shard_map/all_gather | solution.py:124
  113.6 11.0 %copy-start.7 = (bf16[8,256,128]{2,1,0:T(8,128)(2,1)}, bf16[8,256,128]{2,1,0:T(8,128)(2,1)S(1)}, u32[]{:S(2)}) copy-start(bf16[8,256,128]{2,1,0:T(8,128)(2,1)S(1)} %convolution_convert_fusion.1) | copy-start | bytes 1572868
  136.3 14.5 %all-to-all-start.1 = ((f32[32,3,1]{1,2,0:T(1,128)}), f32[32,3,1]{1,2,0:T(1,128)S(1)}, u32[]{:S(2)}, u32[]{:S(2)}) async-start(f32[32,3,1]{1,2,0:T(1,128)} %broadcast_in_dim.23), calls=%async_computation.1 | async-start | bytes 32768 | tf_op jit(solution)/shard_map/all_to_all | solution.py:28
  150.8 21.0 %all-to-all-start.3 = ((bf16[32,8,8,128]{3,1,2,0:T(8,128)(2,1)}), bf16[32,8,8,128]{3,1,2,0:T(8,128)(2,1)S(1)}, u32[]{:S(2)}, u32[]{:S(2)}) async-start(bf16[32,8,8,128]{3,1,2,0:T(8,128)(2,1)} %constant_dynamic-update-slice_fusion), calls=%async_computation.3 | async-start | bytes 1048576 | tf_op jit(solution)/shard_map/all_to_all | solution.py:15
  157.4 21.6 %copy-start.9 = (f32[64]{0:T(128)S(1)}, f32[64]{0:T(128)}, u32[]{:S(2)}) copy-start(f32[64]{0:T(128)} %param.8) | copy-start | bytes 772
  171.8 22.3 %all-to-all-start.2 = ((bf16[256,8,128]{2,1,0:T(8,128)(2,1)}), bf16[256,8,128]{2,1,0:T(8,128)(2,1)S(1)}, u32[]{:S(2)}, u32[]{:S(2)}) async-start(bf16[256,8,128]{2,1,0:T(8,128)(2,1)} %copy.87), calls=%async_computation.2 | async-start | bytes 1048576 | tf_op jit(solution)/shard_map/all_to_all | solution.py:168
  197.8 2.2 copy-start.3
  199.1 1.0 copy-start.1
  293.9 11.0 %copy-start.8 = (bf16[8,256,128]{2,1,0:T(8,128)(2,1)}, bf16[8,256,128]{2,1,0:T(8,128)(2,1)S(1)}, u32[]{:S(2)}) copy-start(bf16[8,256,128]{2,1,0:T(8,128)(2,1)S(1)} %convolution_convert_fusion) | copy-start | bytes 1572868
  315.9 22.5 %all-to-all-start.6 = ((bf16[32,8,8,128]{3,1,2,0:T(8,128)(2,1)}), bf16[32,8,8,128]{3,1,2,0:T(8,128)(2,1)S(1)}, u32[]{:S(2)}, u32[]{:S(2)}) async-start(bf16[32,8,8,128]{3,1,2,0:T(8,128)(2,1)} %constant_dynamic-update-slice_fusion.32), calls=%async_computation.6 | async-start | bytes 1048576 | tf_op jit(solution)/shard_map/all_to_all | solution.py:15
  338.4 0.8 copy-start.5
  339.2 23.2 %all-to-all-start.5 = ((bf16[256,8,128]{2,1,0:T(8,128)(2,1)}), bf16[256,8,128]{2,1,0:T(8,128)(2,1)}, u32[]{:S(2)}, u32[]{:S(2)}) async-start(bf16[256,8,128]{2,1,0:T(8,128)(2,1)} %copy.103), calls=%async_computation.5 | async-start | bytes 1048576 | tf_op jit(solution)/shard_map/all_to_all | solution.py:168
  345.8 18.8 %copy-start.4 = (f32[8,256,128]{2,1,0:T(8,128)S(1)}, f32[8,256,128]{2,1,0:T(8,128)}, u32[]{:S(2)}) copy-start(f32[8,256,128]{2,1,0:T(8,128)} %copy-done.3) | copy-start | bytes 3145732
  364.6 3.1 copy-start.2
  364.6 3.1 copy-start.6
Sparse Core Ops, SparseCore 0:
  32.5 72.3 all-gather.1
